TPU v7x, 512 devices: a whole 4x8x8 slice. The times are simulated.
512 devices in a mesh: dp: 32 (over x, y), mx: 4 (over z_hi, core), my: 4 (over z_lo).
Axes of the slice: x: 4, y: 8, z: 8 (z_hi: 2, z_lo: 4; z = z_hi * 4 + z_lo), core: 2. Of those that a mesh axis runs over, the one named last changes fastest.
Arguments:
- mentor_final_states: bfloat16 [2048, 4608], P('dp'), may hold values from -12 to 12
- mentor_output_matrix: bfloat16 [4608, 4096], P(None, ('mx', 'my')), may hold values from -0.09375 to 0.09375
- learner_final_states: bfloat16 [2048, 3584], P('dp', 'mx'), may hold values from -12 to 12
- learner_output_matrix: bfloat16 [3584, 4096], P('mx', 'my'), may hold values from -0.09375 to 0.09375
- loss_mask: int32 [2048], P('dp'), may hold values 0 or 1
Outputs:
- mismatch_per_piece: float32 [2048], P('dp')
- mean_loss: float32 [], replicated
- student_grad: float32 [2048, 4096], P('dp', 'my')
All inputs are finite; a program needn't handle non-finite values.
Results may differ from a plain program's by a relative error of at most 0.0003.
Values sent between devices are 32-bit elements.
No kernel may reach another device: no remote copies, remote signals or barrier semaphores. Data moves between devices by JAX's collectives and lax.ppermute only.
A program may use at most 64 MiB of HBM per device.

v0:
```python
import jax
import jax.numpy as jnp
from jax import lax
from jax.sharding import Mesh
from jax.sharding import PartitionSpec as P

DP = ("dp_0", "dp_1")
SOFTENING_HEAT = 2.0


def over_axes(array, axes):
    for axis in axes:
        array = lax.psum(array, axis)
    return array


def over_pieces(array, axis):
    blocks = lax.all_gather(array, axis)
    return blocks.sum(axis=0)


def merged(part, axis, combine):
    gathered = jax.tree.map(lambda a: lax.all_gather(a, axis), part)

    def take(source):
        return jax.tree.map(lambda a: lax.dynamic_index_in_dim(a, source, 0, False), gathered)

    return lax.fori_loop(
        1, lax.axis_size(axis), lambda source, state: combine(state, take(source)), take(0)
    )


def picked(array, axis, root):
    return lax.dynamic_index_in_dim(lax.all_gather(array, axis), root, 0, keepdims=False)


def row_stats(values):
    row_max = jnp.max(values, axis=1)
    row_sum = jnp.sum(jnp.exp(values - row_max[:, None]), axis=1)
    return (row_max, row_sum)


def join_stats(left_stat, right_stat):
    row_max = jnp.maximum(left_stat[0], right_stat[0])
    row_sum = left_stat[1] * jnp.exp(left_stat[0] - row_max) + right_stat[1] * jnp.exp(
        right_stat[0] - row_max
    )
    return (row_max, row_sum)


def local(
    mentor_final_states,
    mentor_output_matrix,
    learner_final_states,
    learner_output_matrix,
    loss_mask,
):
    groups = lax.axis_size(("mx", "my"))
    piece_cols = mentor_output_matrix.shape[1]
    lexicon_length = piece_cols * groups
    local_tokens = mentor_final_states.shape[0]
    piece_count = local_tokens * lax.axis_size(DP)
    global_multiplier = SOFTENING_HEAT * lexicon_length * piece_count
    mentor_softened_scores = (
        jnp.dot(mentor_final_states, mentor_output_matrix, preferred_element_type=jnp.float32)
        / SOFTENING_HEAT
    )
    learner_contribution = jnp.dot(
        learner_final_states, learner_output_matrix, preferred_element_type=jnp.float32
    )
    piece_importance = loss_mask.astype(jnp.float32)
    usable_count = over_axes(jnp.sum(piece_importance), DP)
    learner_softened_scores = over_pieces(learner_contribution, "mx") / SOFTENING_HEAT
    teacher_max, teacher_sum = merged(row_stats(mentor_softened_scores), ("mx", "my"), join_stats)
    student_max, student_sum = merged(row_stats(learner_softened_scores), "my", join_stats)
    mentor_logarithmic_odds = mentor_softened_scores - (teacher_max + jnp.log(teacher_sum))[:, None]
    learner_logarithmic_odds = (
        learner_softened_scores - (student_max + jnp.log(student_sum))[:, None]
    )
    outer_block = lax.all_gather(mentor_logarithmic_odds, "my", axis=1, tiled=True)
    aligned = picked(outer_block, "mx", lax.axis_index("my"))
    mentor_likelihoods = jnp.exp(aligned)
    partial_kl = jnp.sum(mentor_likelihoods * (aligned - learner_logarithmic_odds), axis=1)
    mismatch_per_piece = SOFTENING_HEAT * SOFTENING_HEAT * over_pieces(partial_kl, "my")
    prob_gap = jnp.exp(learner_logarithmic_odds) - mentor_likelihoods
    loss_sum = over_axes(jnp.sum(piece_importance * mismatch_per_piece), DP)
    mean_loss = loss_sum / usable_count
    multiplier = piece_importance * global_multiplier / usable_count
    student_grad = prob_gap * multiplier[:, None]
    return (mismatch_per_piece, mean_loss, student_grad)


def solution(mesh):
    split = Mesh(
        mesh.devices.reshape(4, 8, mesh.shape["mx"], mesh.shape["my"]), ("dp_0", "dp_1", "mx", "my")
    )
    in_specs = (P(DP, None), P(None, ("mx", "my")), P(DP, "mx"), P("mx", "my"), P(DP))
    out_specs = (P(DP), P(), P(DP, "my"))
    return jax.shard_map(local, mesh=split, in_specs=in_specs, out_specs=out_specs, check_vma=False)
```

profile of v0, /device:TPU:8, one launch (start us, length us, event | category | flops | bytes accessed | tf_op | source)
XLA Modules:
  0.0 155.5 jit_solution(621932956250404681)
XLA Ops:
  7.2 0.0 copy-start
  7.2 0.0 copy-start.1
  7.2 0.0 all-gather.12.cloned.1.call-start
  7.2 2.9 %fusion.7 = f32[64,1024]{1,0:T(8,128)} fusion(bf16[64,896]{1,0:T(8,128)(2,1)} %param.11, bf16[896,1024]{1,0:T(8,128)(2,1)} %param.12), kind=kOutput, calls=%fused_computation.29 | convolution fusion | flops 117440512 | bytes 2211840 | tf_op jit(solution)/shard_map/dot_general | solution.py:68
  10.1 0.0 all-gather.12.cloned.1.call-update
  10.1 0.0 all-gather.10.cloned.1.call-start
  10.2 0.0 copy-done
  10.2 0.0 copy-done.1
  10.2 0.6 fusion.6
  10.8 0.0 copy-start.2
  10.8 0.2 exponential_reduce_fusion.1
  11.0 1.3 dynamic-slice
  13.0 0.2 dynamic-update-slice
  13.2 0.2 dynamic-update-slice.1
  13.4 40.3 %all-reduce.5 = (f32[1024]{0:T(1024)S(1)}, f32[1024]{0:T(1024)S(1)}) all-reduce(f32[1024]{0:T(1024)S(1)} %dynamic-update-slice, f32[1024]{0:T(1024)S(1)} %dynamic-update-slice.1), channel_id=2, replica_groups=mesh['dp_0'=4,'dp_1'=8,'mx'=4,'my'=4] {'mx','my'}, use_global_device_ids=true, to_apply=%add | all-reduce | flops 2048 | bytes 16384
  53.7 0.1 reshape.11
  53.8 0.1 reshape.12
  53.9 0.7 while.34
  54.5 0.1 broadcast_subtract_fusion
  54.6 15.3 %all_gather.49 = f32[64,1024]{1,0:T(8,128)} all-gather(f32[64,256]{1,0:T(8,128)S(1)} %broadcast_subtract_fusion), channel_id=1, replica_groups=mesh['dp_0'=4,'dp_1'=8,'mx'=4,'my'=4] {'my'}, dimensions={1}, use_global_device_ids=true | all-gather | bytes 327680 | tf_op jit(solution)/shard_map/all_gather | solution.py:80
  69.9 0.0 all-gather.10.cloned.1.call-update
  69.9 1.3 dynamic-slice.2
  71.9 0.0 all-gather.12.cloned.1.call-done
  71.9 1.3 reduce_sum.64
  73.2 0.1 multiply_reduce_fusion
  73.3 0.2 dynamic-update-slice.2
  73.6 0.2 exponential_reduce_fusion
  73.8 0.2 dynamic-update-slice.3
  74.0 8.7 %all-reduce.7 = (f32[256]{0:T(256)S(1)}, f32[256]{0:T(256)S(1)}) all-reduce(f32[256]{0:T(256)S(1)} %dynamic-update-slice.2, f32[256]{0:T(256)S(1)} %dynamic-update-slice.3), channel_id=6, replica_groups=mesh['dp_0'=4,'dp_1'=8,'mx'=4,'my'=4] {'my'}, use_global_device_ids=true, to_apply=%add.2 | all-reduce | flops 512 | bytes 4096
  82.7 0.1 reshape.15
  82.8 0.1 reshape.16
  82.9 0.1 while.35
  83.0 21.3 %all-gather.10.cloned.1.call-done = f32[256,1024]{1,0:T(8,128)} async-done(((f32[64,1024]{1,0:T(8,128)}), f32[256,1024]{1,0:T(8,128)}) %all-gather.10.cloned.1.call-update) | async-done | bytes 1048592 | tf_op jit(solution)/shard_map/all_gather | solution.py:34
  104.4 1.2 fusion.5
  105.5 0.2 dynamic-update-slice.4
  105.8 9.3 %all-reduce.4 = f32[256]{0:T(256)S(1)} all-reduce(f32[256]{0:T(256)S(1)} %dynamic-update-slice.4), channel_id=8, replica_groups=mesh['dp_0'=4,'dp_1'=8,'mx'=4,'my'=4] {'my'}, use_global_device_ids=true, to_apply=%add.4 | all-reduce | flops 256 | bytes 2048
  115.1 0.1 reshape.17
  115.2 0.0 copy-done.2
  115.2 1.1 convert_reduce_fusion
  116.3 11.0 %all-reduce.8 = (f32[]{:T(128)}, f32[]{:T(128)}) all-reduce(f32[]{:T(128)} %get-tuple-element.274, f32[]{:T(128)} %get-tuple-element.273), channel_id=1, replica_groups=mesh['dp_0'=4,'dp_1'=8,'mx'=4,'my'=4] {'dp_0'}, use_global_device_ids=true, to_apply=%region_12.13 | all-reduce | flops 2 | bytes 16 | tf_op jit(solution)/shard_map/psum | solution.py:13
  127.3 16.4 %all-reduce.6 = (f32[]{:T(128)}, f32[]{:T(128)}) all-reduce(f32[]{:T(128)} %get-tuple-element.301, f32[]{:T(128)} %get-tuple-element.302), channel_id=1, replica_groups=mesh['dp_0'=4,'dp_1'=8,'mx'=4,'my'=4] {'dp_1'}, use_global_device_ids=true, to_apply=%region_13.14 | all-reduce | flops 2 | bytes 16 | tf_op jit(solution)/shard_map/psum | solution.py:13
  143.8 0.6 multiply_divide_fusion
  144.4 1.8 %subtract_multiply_fusion = f32[64,1024]{1,0:T(8,128)} fusion(f32[4,64,1024]{2,1,0:T(8,128)} %bitcast.49, s32[]{:T(128)S(6)} %select_n.32, f32[64,1024]{1,0:T(8,128)S(1)} %reduce_sum.64, f32[64]{0:T(128)S(1)} %multiply_divide_fusion, f32[64]{0:T(128)S(1)} %log_add_fusion), kind=kLoop, calls=%fused_computation.17 | loop fusion | flops 262144 | bytes 786948 | tf_op jit(solution)/shard_map/mul | solution.py:89
  (30 shorter events, 0.5 us)
Async XLA Ops:
  7.2 3.0 %copy-start = (bf16[4608,256]{1,0:T(8,128)(2,1)S(1)}, bf16[4608,256]{1,0:T(8,128)(2,1)}, u32[]{:S(2)}) copy-start(bf16[4608,256]{1,0:T(8,128)(2,1)} %param.10) | copy-start | bytes 7077892
  7.2 3.0 %copy-start.1 = (bf16[64,4608]{1,0:T(8,128)(2,1)S(1)}, bf16[64,4608]{1,0:T(8,128)(2,1)}, u32[]{:S(2)}) copy-start(bf16[64,4608]{1,0:T(8,128)(2,1)} %param.9) | copy-start | bytes 1769476
  7.2 64.7 %all-gather.12.cloned.1.call-start = ((), (), s32[]{:S(2)}) async-start(), calls=%async_computation.1 | async-start | bytes 1310720 | tf_op jit(solution)/shard_map/all_gather | solution.py:18
  10.1 94.2 %all-gather.10.cloned.1.call-start = ((), (), s32[]{:S(2)}) async-start(), calls=%async_computation | async-start | bytes 1310720 | tf_op jit(solution)/shard_map/all_gather | solution.py:34
  10.8 104.4 %copy-start.2 = (s32[64]{0:T(128)S(1)}, s32[64]{0:T(128)}, u32[]{:S(2)}) copy-start(s32[64]{0:T(128)} %param.13) | copy-start | bytes 772
Sparse Core Ops, SparseCore 0:
  10.7 39.8 all-gather.11
  70.1 34.2 all-gather.9
where the time goes:
time: 156 us
  blocking collectives  101 us (65%)
  waiting for transfers between devices  21.4 us (14%)
  between operations  18 us (12%)
  other arithmetic  7.11 us (5%)
  local copies, waits for them, and re-layouts  4.15 us (3%)
  matrix products  3.48 us (2%)
    unnamed x3, blocking collectives  58.3 us
    psum x2, blocking collectives, over_axes(): array = lax.psum(array, axis)  27.4 us
    all_gather x1, waiting for transfers between devices, picked(): lax.all_gather(array, axis)  21.3 us
    all_gather x1, blocking collectives, local(): lax.all_gather(mentor_logarithmic_odds, 'my', axis=1, tiled=True)  15.3 us
    unnamed x18, local copies, waits for them, and re-layouts  3.76 us
  transfers between devices with their start and end apart: 2, of which 1 were waited for; matrix products, arithmetic and copies ran while one was open for 4% of the time, Pallas kernels for 0%

commit v1 on v0

--- a/solution.py
+++ b/solution.py
@@ -10,7 +10,7 @@
 
 def over_axes(array, axes):
     for axis in axes:
-        array = lax.psum(array, axis)
+        array = jnp.sum(lax.all_gather(array, axis), axis=0)
     return array
 
 

time: 156 us -> 164 us (1.051)
  local copies, waits for them, and re-layouts: 4.15 us -> 12.2 us
  other arithmetic: 7.11 us -> 9.71 us
    psum x2 -> x0, blocking collectives: 27.4 us -> none  [over_axes(): array = lax.psum(array, axis)]
    unnamed x3 -> x5, blocking collectives: 58.3 us -> 84.7 us
    unnamed x18 -> x28, local copies, waits for them, and re-layouts: 3.76 us -> 11.8 us
    reduce_sum x0 -> x4, other arithmetic: none -> 2.56 us  [over_axes(): array = jnp.sum(lax.all_gather(array, axis), axis=0)]
  transfers between devices with their start and end apart: 2 -> 2, of which waited for: 1 -> 1; matrix products, arithmetic and copies ran while one was open for 4% -> 5% of each run, Pallas kernels for 0% -> 0%
where the time goes in v1:
time: 164 us
  blocking collectives  99.8 us (61%)
  waiting for transfers between devices  20 us (12%)
  between operations  18 us (11%)
  local copies, waits for them, and re-layouts  12.2 us (7%)
  other arithmetic  9.71 us (6%)
  matrix products  3.48 us (2%)
    unnamed x5, blocking collectives  84.7 us
    all_gather x1, waiting for transfers between devices, picked(): lax.all_gather(array, axis)  20 us
    all_gather x1, blocking collectives, local(): lax.all_gather(mentor_logarithmic_odds, 'my', axis=1, tiled=True)  15.1 us
    unnamed x28, local copies, waits for them, and re-layouts  11.8 us
  transfers between devices with their start and end apart: 2, of which 1 were waited for; matrix products, arithmetic and copies ran while one was open for 5% of the time, Pallas kernels for 0%

profile of v1, /device:TPU:8, one launch (start us, length us, event | category | flops | bytes accessed | tf_op | source)
XLA Modules:
  0.0 163.6 jit_solution(7547707529276238383)
XLA Ops:
  7.2 0.0 copy-start
  7.2 0.0 all-gather.12.cloned.1.call-start
  7.2 2.9 %fusion.7 = f32[64,1024]{1,0:T(8,128)} fusion(bf16[64,896]{1,0:T(8,128)(2,1)} %param.11, bf16[896,1024]{1,0:T(8,128)(2,1)} %param.12), kind=kOutput, calls=%fused_computation.29 | convolution fusion | flops 117440512 | bytes 2211840 | tf_op jit(solution)/shard_map/dot_general | solution.py:68
  10.1 0.0 all-gather.12.cloned.1.call-update
  10.1 0.0 all-gather.10.cloned.1.call-start
  10.2 1.3 dynamic-slice
  12.1 0.6 fusion.6
  12.7 0.0 copy-start.2
  12.8 0.2 exponential_reduce_fusion.1
  12.9 0.2 dynamic-update-slice
  13.2 0.2 dynamic-update-slice.1
  13.4 40.3 %all-reduce.9 = (f32[1024]{0:T(1024)S(1)}, f32[1024]{0:T(1024)S(1)}) all-reduce(f32[1024]{0:T(1024)S(1)} %dynamic-update-slice, f32[1024]{0:T(1024)S(1)} %dynamic-update-slice.1), channel_id=2, replica_groups=mesh['dp_0'=4,'dp_1'=8,'mx'=4,'my'=4] {'mx','my'}, use_global_device_ids=true, to_apply=%add | all-reduce | flops 2048 | bytes 16384
  53.7 0.1 reshape.11
  53.8 0.1 reshape.12
  53.9 0.7 while.34
  54.6 0.1 broadcast_subtract_fusion
  54.6 15.1 %all_gather.73 = f32[64,1024]{1,0:T(8,128)} all-gather(f32[64,256]{1,0:T(8,128)S(1)} %broadcast_subtract_fusion), channel_id=1, replica_groups=mesh['dp_0'=4,'dp_1'=8,'mx'=4,'my'=4] {'my'}, dimensions={1}, use_global_device_ids=true | all-gather | bytes 327680 | tf_op jit(solution)/shard_map/all_gather | solution.py:80
  69.8 0.0 all-gather.10.cloned.1.call-update
  69.8 1.3 dynamic-slice.2
  71.7 1.3 dynamic-slice.5
  73.0 1.3 reduce_sum.100
  74.3 0.1 multiply_reduce_fusion
  74.4 0.2 dynamic-update-slice.2
  74.7 0.2 exponential_reduce_fusion
  74.9 0.2 dynamic-update-slice.3
  75.1 9.0 %all-reduce.11 = (f32[256]{0:T(256)S(1)}, f32[256]{0:T(256)S(1)}) all-reduce(f32[256]{0:T(256)S(1)} %dynamic-update-slice.2, f32[256]{0:T(256)S(1)} %dynamic-update-slice.3), channel_id=6, replica_groups=mesh['dp_0'=4,'dp_1'=8,'mx'=4,'my'=4] {'my'}, use_global_device_ids=true, to_apply=%add.2 | all-reduce | flops 512 | bytes 4096
  84.1 0.1 reshape.15
  84.2 0.1 reshape.16
  84.2 0.1 while.35
  84.4 20.0 %all-gather.10.cloned.1.call-done = f32[256,1024]{1,0:T(8,128)} async-done(((f32[64,1024]{1,0:T(8,128)}), f32[256,1024]{1,0:T(8,128)}) %all-gather.10.cloned.1.call-update) | async-done | bytes 1048592 | tf_op jit(solution)/shard_map/all_gather | solution.py:34
  104.4 1.2 fusion.5
  105.5 0.2 dynamic-update-slice.4
  105.8 9.3 %all-reduce.4 = f32[256]{0:T(256)S(1)} all-reduce(f32[256]{0:T(256)S(1)} %dynamic-update-slice.4), channel_id=8, replica_groups=mesh['dp_0'=4,'dp_1'=8,'mx'=4,'my'=4] {'my'}, use_global_device_ids=true, to_apply=%add.4 | all-reduce | flops 256 | bytes 2048
  115.1 0.1 reshape.17
  115.2 1.1 convert_reduce_fusion
  116.3 1.3 dynamic-update-slice.7
  117.6 1.3 dynamic-update-slice.5
  119.0 1.3 dynamic-slice.6
  120.2 10.4 %all-reduce.12 = (f32[4]{0:T(128)S(1)}, f32[4]{0:T(128)S(1)}) all-reduce(f32[4]{0:T(128)S(1)} %dynamic-update-slice.5, f32[4]{0:T(128)S(1)} %dynamic-update-slice.7), channel_id=1, replica_groups=mesh['dp_0'=4,'dp_1'=8,'mx'=4,'my'=4] {'dp_0'}, use_global_device_ids=true, to_apply=%add.5 | all-reduce | flops 8 | bytes 64
  130.6 0.7 reduce_sum.108
  131.3 0.6 reduce_sum.105
  131.9 1.4 dynamic-update-slice.8
  133.3 1.4 dynamic-update-slice.6
  134.7 15.7 %all-reduce.10 = (f32[8]{0:T(128)S(1)}, f32[8]{0:T(128)S(1)}) all-reduce(f32[8]{0:T(128)S(1)} %dynamic-update-slice.6, f32[8]{0:T(128)S(1)} %dynamic-update-slice.8), channel_id=1, replica_groups=mesh['dp_0'=4,'dp_1'=8,'mx'=4,'my'=4] {'dp_1'}, use_global_device_ids=true, to_apply=%add.6 | all-reduce | flops 16 | bytes 128
  150.5 0.7 reduce_sum.109
  151.1 0.7 multiply_divide_fusion
  151.8 1.8 %subtract_multiply_fusion = f32[64,1024]{1,0:T(8,128)} fusion(f32[4,64,1024]{2,1,0:T(8,128)} %bitcast.55, s32[]{:T(128)S(6)} %select_n.32, f32[64,1024]{1,0:T(8,128)S(1)} %reduce_sum.100, f32[64]{0:T(128)S(1)} %multiply_divide_fusion, f32[64]{0:T(128)S(1)} %log_add_fusion), kind=kLoop, calls=%fused_computation.17 | loop fusion | flops 262144 | bytes 786948 | tf_op jit(solution)/shard_map/mul | solution.py:89
  153.6 0.6 reduce_sum.106
  (39 shorter events, 0.6 us)
Async XLA Ops:
  7.2 4.9 %copy-start = (bf16[4608,256]{1,0:T(8,128)(2,1)S(1)}, bf16[4608,256]{1,0:T(8,128)(2,1)}, u32[]{:S(2)}) copy-start(bf16[4608,256]{1,0:T(8,128)(2,1)} %param.10) | copy-start | bytes 7077892
  7.2 4.9 %copy-start.1 = (bf16[64,4608]{1,0:T(8,128)(2,1)S(1)}, bf16[64,4608]{1,0:T(8,128)(2,1)}, u32[]{:S(2)}) copy-start(bf16[64,4608]{1,0:T(8,128)(2,1)} %param.9) | copy-start | bytes 1769476
  7.2 65.8 %all-gather.12.cloned.1.call-start = ((), (), s32[]{:S(2)}) async-start(), calls=%async_computation.1 | async-start | bytes 1310720 | tf_op jit(solution)/shard_map/all_gather | solution.py:18
  10.1 94.3 %all-gather.10.cloned.1.call-start = ((), (), s32[]{:S(2)}) async-start(), calls=%async_computation | async-start | bytes 1310720 | tf_op jit(solution)/shard_map/all_gather | solution.py:34
  12.7 102.5 %copy-start.2 = (s32[64]{0:T(128)S(1)}, s32[64]{0:T(128)}, u32[]{:S(2)}) copy-start(s32[64]{0:T(128)} %param.13) | copy-start | bytes 772
Sparse Core Ops, SparseCore 0:
  10.7 39.8 all-gather.11
  69.9 34.4 all-gather.9
